TPU v7x, 32 devices: a whole 2x2x4 slice. The times are simulated.
32 devices in a mesh: seq: 8 (over y, x, core), tp: 4 (over z).
Axes of the slice: x: 2, y: 2, z: 4, core: 2. Of those that a mesh axis runs over, the one named last changes fastest.
Arguments:
- hidden: bfloat16 [4096, 4096], P('seq', 'tp'), may hold values from -6 to 6
- norm_gain: float32 [4096], P('tp'), may hold values from 0.5 to 1.5
- rank_down: bfloat16 [4096, 1024], P('tp'), may hold values from -0.09375 to 0.09375
- gate_up: bfloat16 [1024, 4096], P(None, 'tp'), may hold values from -0.1875 to 0.1875
- value_up: bfloat16 [1024, 4096], P(None, 'tp'), may hold values from -0.1875 to 0.1875
- state_up: bfloat16 [1024, 1024], P(None, 'tp'), may hold values from -0.1875 to 0.1875
- step_up: bfloat16 [1024, 64], P(None, 'tp'), may hold values from -0.1875 to 0.1875
- conv_value: float32 [4, 4096], P(None, 'tp'), may hold values from -3 to 3
- conv_state: float32 [4, 1024], P(None, 'tp'), may hold values from -3 to 3
- step_bias: float32 [64], P('tp'), may hold values from -6.9 to -2.3
- decay_log: float32 [64], P('tp'), may hold values from -11 to 2.77
- skip_gain: float32 [64], P('tp'), may hold values from 0.5 to 1.5
- gate_gain: float32 [4096], P('tp'), may hold values from 0.5 to 1.5
- out_down: bfloat16 [4096, 1024], P('tp'), may hold values from -0.09375 to 0.09375
- out_up: bfloat16 [1024, 4096], P(None, 'tp'), may hold values from -0.1875 to 0.1875
Outputs:
- block_out: bfloat16 [4096, 4096], P('seq', 'tp')
All inputs are finite; a program needn't handle non-finite values.
Results may differ from a plain program's by a relative error of at most 0.012.
Values may be sent and summed in bfloat16 or wider, within the bound.
A program may use at most 64 MiB of HBM per device.

v0:
```python
import jax
import jax.numpy as jnp
from jax import lax
from jax.sharding import PartitionSpec as P

HEAD_DIM = 64
NSTATE = 128
GROUPS = 4
epsilon = 1e-05
highest = lax.Precision.HIGHEST


def shifted(shard, axis, by):
    peers = lax.axis_size(axis)
    pairs = [(i, i + by) for i in range(peers) if 0 <= i + by < peers]
    return lax.ppermute(shard, axis, pairs)


def entering(part, axis, combine, identity):
    place = lax.axis_index(axis)
    gathered = jax.tree.map(lambda a: lax.all_gather(a, axis), part)
    state = jax.tree.map(lambda a, e: jnp.zeros_like(a) + jnp.asarray(e, a.dtype), part, identity)

    def one(lap, state):
        return combine(
            state, jax.tree.map(lambda a: lax.dynamic_index_in_dim(a, lap, 0, False), gathered)
        )

    return lax.fori_loop(0, place, one, state)


def contract_rows(left, right):
    return lax.dot_general(
        left, right, (((0,), (0,)), ((), ())), preferred_element_type=jnp.float32
    )


def contract_columns(columns, rows):
    return lax.dot_general(
        columns, rows, (((0,), (1,)), ((), ())), preferred_element_type=jnp.float32
    )


def depthwise(rim_rows, current, weights):
    joined = jnp.concatenate([rim_rows, current], axis=0).astype(jnp.float32)
    length = current.shape[0]
    result = jnp.zeros(current.shape, jnp.float32)
    for offset in range(weights.shape[0]):
        result = result + weights[offset] * joined[offset : offset + length]
    return jax.nn.silu(result).astype(jnp.bfloat16)


def on_device(
    hidden,
    norm_gain,
    rank_down,
    gate_up,
    value_up,
    state_up,
    step_up,
    conv_value,
    conv_state,
    step_bias,
    decay_log,
    skip_gain,
    gate_gain,
    out_down,
    out_up,
):
    tokens = hidden.shape[0]
    tp_count = lax.axis_size("tp")
    tp_index = lax.axis_index("tp")
    model_width = hidden.shape[1] * tp_count
    hidden_wide = hidden.astype(jnp.float32)
    local_squares = jnp.sum(hidden_wide * hidden_wide, axis=1)
    scaled = (hidden_wide * norm_gain).astype(jnp.bfloat16)
    up_weights = (gate_up, value_up, state_up, step_up)
    partial_value = jnp.dot(scaled, rank_down, preferred_element_type=jnp.float32)
    summed, total_squares = lax.psum((partial_value, local_squares), "tp")
    factor = lax.rsqrt(total_squares / model_width + epsilon)
    reduced = (summed * factor[:, None]).astype(jnp.bfloat16)
    projected = tuple(
        (jnp.dot(reduced, weight, preferred_element_type=jnp.float32) for weight in up_weights)
    )
    gate_pre = projected[0].astype(jnp.bfloat16)
    value_pre = projected[1].astype(jnp.bfloat16)
    state_pre = projected[2].astype(jnp.bfloat16)
    step_pre = projected[3].astype(jnp.bfloat16)
    rim_start = tokens - conv_value.shape[0] + 1
    rim_value, rim_state = shifted((value_pre[rim_start:], state_pre[rim_start:]), "seq", 1)
    value_act = depthwise(rim_value, value_pre, conv_value)
    state_act = depthwise(rim_state, state_pre, conv_state)
    state_all = lax.all_gather(state_act, "tp", axis=1, tiled=True)
    heads_local = decay_log.shape[0]
    heads_total = heads_local * tp_count
    group_index = tp_index * heads_local // (heads_total // GROUPS)
    inward = lax.dynamic_slice_in_dim(state_all, group_index * NSTATE, NSTATE, 1).astype(
        jnp.float32
    )
    outward = lax.dynamic_slice_in_dim(
        state_all, (GROUPS + group_index) * NSTATE, NSTATE, 1
    ).astype(jnp.float32)
    step_size = jax.nn.softplus(step_pre.astype(jnp.float32) + step_bias)
    log_decay = jnp.cumsum(-jnp.exp(decay_log) * step_size, axis=0)
    values = value_act.astype(jnp.float32).reshape(tokens, heads_local, HEAD_DIM)
    coupling = jnp.dot(outward, inward.T, precision=highest)
    positions = jnp.arange(tokens)
    causal = positions[:, None] >= positions[None, :]
    spread = log_decay.T[:, :, None] - log_decay.T[:, None, :]
    attenuation = jnp.where(causal[None], jnp.exp(jnp.where(causal[None], spread, 0.0)), 0.0)
    mixing = coupling[None] * attenuation * step_size.T[:, None, :]
    within = jnp.einsum("hts,shp->thp", mixing, values, precision=highest)
    ending = jnp.exp(log_decay[-1][None, :] - log_decay) * step_size
    local_state = jnp.einsum("sh,shp,sn->hpn", ending, values, inward, precision=highest)
    local_decay = jnp.exp(log_decay[-1])

    def combine(earlier, later):
        return (earlier[0] * later[0], later[0][:, None, None] * earlier[1] + later[1])

    prefix = entering(
        (local_decay, local_state),
        "seq",
        combine,
        (jnp.ones_like(local_decay), jnp.zeros_like(local_state)),
    )
    incoming = prefix[1]
    carried_in = jnp.exp(log_decay)[:, :, None] * jnp.einsum(
        "tn,hpn->thp", outward, incoming, precision=highest
    )
    mixed = (within + carried_in + skip_gain[None, :, None] * values).reshape(
        tokens, heads_local * HEAD_DIM
    )
    gated = mixed * jax.nn.silu(gate_pre.astype(jnp.float32))
    group_width = heads_total * HEAD_DIM // GROUPS
    selector = (jnp.arange(GROUPS) == group_index).astype(jnp.float32)
    group_sums = lax.psum(jnp.sum(gated * gated, axis=1)[:, None] * selector[None, :], "tp")
    own_sum = jnp.sum(group_sums * selector[None, :], axis=1)
    normed = (gated * lax.rsqrt(own_sum / group_width + epsilon)[:, None] * gate_gain).astype(
        jnp.bfloat16
    )
    out_share = lax.psum_scatter(
        contract_columns(out_down, normed), "tp", scatter_dimension=0, tiled=True
    ).astype(jnp.bfloat16)
    update = contract_rows(lax.all_gather(out_share, "tp", axis=0, tiled=True), out_up)
    return (hidden_wide + update).astype(jnp.bfloat16)


def solution(mesh):
    return jax.shard_map(
        on_device,
        mesh=mesh,
        in_specs=(
            P("seq", "tp"),
            P("tp"),
            P("tp", None),
            P(None, "tp"),
            P(None, "tp"),
            P(None, "tp"),
            P(None, "tp"),
            P(None, "tp"),
            P(None, "tp"),
            P("tp"),
            P("tp"),
            P("tp"),
            P("tp"),
            P("tp", None),
            P(None, "tp"),
        ),
        out_specs=P("seq", "tp"),
        check_vma=False,
    )
```

profile of v0, /device:TPU:0, one launch (start us, length us, event | category | flops | bytes accessed | tf_op | source)
XLA Modules:
  0.0 310.0 jit_solution(9953234598632457863)
XLA Ops:
  6.5 4.6 %fusion.29 = f32[512,1024]{1,0:T(8,128)} fusion(bf16[1024,1024]{1,0:T(8,128)(2,1)} %param.19, bf16[512,1024]{1,0:T(8,128)(2,1)} %param.17, f32[1024]{0:T(1024)} %param.18), kind=kOutput, calls=%fused_computation.51 | convolution fusion | flops 1075314688 | bytes 5246976 | tf_op jit(solution)/shard_map/dot_general | solution.py:78
  11.2 0.0 all-gather.6.cloned.1.call-start
  11.3 1.1 copy-done.4
  12.4 0.3 fusion.20
  12.7 13.9 %psum.22 = f32[512]{0:T(512)S(1)} all-reduce(f32[512]{0:T(512)S(1)} %fusion.20), channel_id=1, replica_groups=mesh['seq'=8,'tp'=4] {'tp'}, use_global_device_ids=true, to_apply=%region_2.0 | all-reduce | flops 512 | bytes 4096 | tf_op jit(solution)/shard_map/psum | solution.py:79
  26.6 0.6 fusion.57
  27.2 73.1 %all-reduce.2.cloned.1.call-done = f32[512,1024]{1,0:T(8,128)} async-done(((f32[512,1024]{1,0:T(8,128)}), f32[512,1024]{1,0:T(8,128)}) %all-reduce.2.cloned.1.call-update) | async-done | bytes 2097168 | tf_op jit(solution)/shard_map/psum | solution.py:79
  100.3 1.8 multiply_convert_fusion.2
  102.2 0.4 fusion.28
  102.6 0.1 compare_select_fusion.1
  102.7 0.4 convolution_convert_fusion.2
  103.1 0.6 slice.90
  103.7 2.0 collective-permute-start.1
  105.7 1.1 reduce-window.6
  106.8 0.2 slice_reduce_fusion
  107.0 0.7 maximum_convert_fusion.1
  107.7 1.7 multiply_convert_fusion.4
  109.5 0.0 all-gather.10.cloned.1.call-start
  109.5 2.8 convolution_convert_fusion.1
  112.4 3.4 %collective-permute-start = (bf16[3,1024]{1,0:T(4,128)(2,1)S(1)}, bf16[3,1024]{1,0:T(4,128)(2,1)S(1)}, u32[]{:S(2)}, u32[]{:S(2)}) collective-permute-start(bf16[3,1024]{1,0:T(4,128)(2,1)S(1)} %slice.85), channel_id=1, source_target_pairs={{0,4},{4,8},{8,12},{12,16},{16,20},{20,24},{24,28},{1,5},{5,9},{9,... | collective-permute-start | bytes 18440 | tf_op jit(solution)/shard_map/ppermute | solution.py:16
  115.8 0.1 copy_bitcast_fusion
  115.9 0.2 slice_reduce_fusion.1
  116.1 0.1 bitcast_exponential_fusion
  116.2 0.4 collective-permute-done
  116.7 0.3 maximum_convert_fusion
  117.0 1.3 multiply_convert_fusion.1
  118.2 1.3 copy.29
  119.6 21.0 %all-gather.6.cloned.1.call-done = bf16[512,1024]{1,0:T(8,128)(2,1)} async-done(((bf16[512,256]{1,0:T(8,128)(2,1)}), bf16[512,1024]{1,0:T(8,128)(2,1)}) %all-gather.6.cloned.1.call-update) | async-done | bytes 1048592 | tf_op jit(solution)/shard_map/all_gather | solution.py:93
  140.6 3.2 %fusion.13 = f32[16,64,128]{2,1,0:T(8,128)} fusion(bf16[512,16,64]{0,2,1:T(8,128)(2,1)} %bitcast.86, f32[512,16]{0,1:T(8,128)S(1)} %get-tuple-element.63, bf16[512,1024]{1,0:T(8,128)(2,1)} %all-gather.6.cloned.1.call-done, s32[]{:T(128)S(6)} %select_n.35), kind=kOutput, calls=%fused_computation.22 | convolution fusion | flops 806354944 | bytes 1736708 | tf_op jit(solution)/shard_map/sh,shp,sn->hpn/dot_general | solution.py:114
  143.8 0.0 reduce-scatter.2.cloned.1.call-start
  143.9 0.1 iota_compare_fusion
  143.9 7.9 %all-gather.1 = f32[8,1,16]{2,1,0:T(1,128)S(1)} all-gather(f32[1,1,16]{2,1,0:T(1,128)S(1)} %bitcast.100), channel_id=1, replica_groups=mesh['seq'=8,'tp'=4] {'seq'}, dimensions={0}, use_global_device_ids=true | all-gather | bytes 576 | tf_op jit(solution)/shard_map/all_gather | solution.py:21
  151.9 2.3 fusion.42
  154.1 24.7 %all-gather.10.cloned.1.call-done = f32[128,64,128]{2,1,0:T(8,128)} async-done(((f32[16,64,128]{2,1,0:T(8,128)}), f32[128,64,128]{2,1,0:T(8,128)}) %all-gather.10.cloned.1.call-update) | async-done | bytes 4194320 | tf_op jit(solution)/shard_map/all_gather | solution.py:21
  178.9 0.2 while.12
  179.1 2.0 fusion.39
  181.2 14.3 %fusion.14 = f32[512,16,64]{0,2,1:T(8,128)} fusion(bf16[512,16,64]{0,2,1:T(8,128)(2,1)S(1)} %bitcast.87, f32[512,16,64]{0,2,1:T(8,128)S(1)} %fusion.39, f32[16,512]{1,0:T(8,128)S(1)} %get-tuple-element.66, f32[16,512]{1,0:T(8,128)S(1)} %get-tuple-element.64, f32[512,512]{1,0:T(8,128)S(1)} %copy-done.6, pred[512,512]{1,0:T(8,128)(4,1)S(1)} %iota_compare_fusion, ...), kind=kOutput, calls=%fused_computation.23 | convolution fusion | flops 3244818432 | bytes 6651968 | tf_op jit(solution)/shard_map/hts,shp->thp/dot_general | solution.py:112
  195.5 3.0 copy.32
  198.5 4.5 %multiply_reduce_fusion = (f32[512]{0:T(512)S(1)}, f32[512,1024]{1,0:T(8,128)}) fusion(f32[512,1024]{1,0:T(8,128)} %copy.32, bf16[512,1024]{1,0:T(8,128)(2,1)S(1)} %copy-done.3, bf16[1024,1024]{1,0:T(8,128)(2,1)S(1)} %copy-done), kind=kOutput, calls=%fused_computation.40 | convolution fusion | flops 1078459904 | bytes 7342080 | tf_op jit(solution)/shard_map/dot_general | solution.py:83
  203.0 0.1 broadcast_multiply_fusion
  203.1 11.8 %psum.23 = f32[512,4]{0,1:T(4,128)S(1)} all-reduce(f32[512,4]{0,1:T(4,128)S(1)} %broadcast_multiply_fusion), channel_id=1, replica_groups=mesh['seq'=8,'tp'=4] {'tp'}, use_global_device_ids=true, to_apply=%region_8.9 | all-reduce | flops 2048 | bytes 16384 | tf_op jit(solution)/shard_map/psum | solution.py:136
  214.9 0.1 multiply_reduce_fusion.1
  215.0 4.8 %convolution_bitcast_fusion = f32[1024,512]{0,1:T(8,128)} fusion(bf16[1024,1024]{1,0:T(8,128)(2,1)} %param.30, f32[512,1024]{1,0:T(8,128)} %get-tuple-element.77, f32[1024]{0:T(1024)S(1)} %copy-done.12, f32[512]{0:T(512)S(1)} %add_rsqrt_fusion), kind=kOutput, calls=%fused_computation.43 | convolution fusion | flops 1075314688 | bytes 6297600 | tf_op jit(solution)/shard_map/dot_general | solution.py:39
  219.9 0.0 all-gather.8.cloned.1.call-start
  219.9 48.4 %reduce-scatter.2.cloned.1.call-done = f32[256,512]{0,1:T(8,128)} async-done(((f32[1024,512]{0,1:T(8,128)}), f32[256,512]{0,1:T(8,128)}) %reduce-scatter.2.cloned.1.call-update) | async-done | bytes 524304 | tf_op jit(solution)/shard_map/reduce_scatter | solution.py:141
  268.3 1.8 convert_element_type.79
  270.1 29.3 %all-gather.8.cloned.1.call-done = bf16[1024,512]{0,1:T(8,128)(2,1)} async-done(((bf16[256,512]{0,1:T(8,128)(2,1)}), bf16[1024,512]{0,1:T(8,128)(2,1)}) %all-gather.8.cloned.1.call-update) | async-done | bytes 1048592 | tf_op jit(solution)/shard_map/all_gather | solution.py:144
  299.4 4.1 %fusion.21 = bf16[512,1024]{1,0:T(8,128)(2,1)} fusion(bf16[512,1024]{1,0:T(8,128)(2,1)S(1)} %copy-done.5, bf16[1024,512]{0,1:T(8,128)(2,1)} %all-gather.8.cloned.1.call-done, bf16[1024,1024]{1,0:T(8,128)(2,1)} %param.31), kind=kOutput, calls=%fused_computation.30 | convolution fusion | flops 1075314688 | bytes 5242880 | tf_op jit(solution)/shard_map/dot_general | solution.py:33
  (46 shorter events, 0.3 us)
Async XLA Ops:
  6.5 192.0 %copy-start = (bf16[1024,1024]{1,0:T(8,128)(2,1)S(1)}, bf16[1024,1024]{1,0:T(8,128)(2,1)}, u32[]{:S(2)}) copy-start(bf16[1024,1024]{1,0:T(8,128)(2,1)} %param.20) | copy-start | bytes 6291460
  6.5 93.8 %all-reduce.2.cloned.1.call-start = ((), (), s32[]{:S(2)}) async-start(), calls=%async_computation.1 | async-start | bytes 4194304 | tf_op jit(solution)/shard_map/psum | solution.py:79
  11.2 1.2 copy-start.4
  11.2 15.4 %copy-start.13 = (f32[16]{0:T(128)S(1)}, f32[16]{0:T(128)}, u32[]{:S(2)}) copy-start(f32[16]{0:T(128)} %param.27) | copy-start | bytes 196
  11.2 15.4 %copy-start.9 = (f32[4,256]{1,0:T(4,128)S(1)}, f32[4,256]{1,0:T(4,128)}, u32[]{:S(2)}) copy-start(f32[4,256]{1,0:T(4,128)} %param.25) | copy-start | bytes 12292
  11.2 16.0 %copy-start.8 = (f32[4,1024]{1,0:T(4,128)S(1)}, f32[4,1024]{1,0:T(4,128)}, u32[]{:S(2)}) copy-start(f32[4,1024]{1,0:T(4,128)} %param.24) | copy-start | bytes 49156
  11.2 129.4 %all-gather.6.cloned.1.call-start = ((), (), s32[]{:S(2)}) async-start(), calls=%async_computation.2 | async-start | bytes 1310720 | tf_op jit(solution)/shard_map/all_gather | solution.py:93
  12.4 89.8 %copy-start.7 = (bf16[1024,16]{0,1:T(8,128)(2,1)S(1)}, bf16[1024,16]{0,1:T(8,128)(2,1)}, u32[]{:S(2)}) copy-start(bf16[1024,16]{0,1:T(8,128)(2,1)} %param.23) | copy-start | bytes 98308
  12.4 89.8 %copy-start.10 = (f32[16]{0:T(128)S(1)}, f32[16]{0:T(128)}, u32[]{:S(2)}) copy-start(f32[16]{0:T(128)} %param.26) | copy-start | bytes 196
  100.3 2.3 copy-start.11
  102.2 7.3 %copy-start.2 = (bf16[512,1024]{1,0:T(8,128)(2,1)}, bf16[512,1024]{1,0:T(8,128)(2,1)S(1)}, u32[]{:S(2)}) copy-start(bf16[512,1024]{1,0:T(8,128)(2,1)S(1)} %multiply_convert_fusion.2) | copy-start | bytes 3145732
  103.7 3.3 %collective-permute-start.1 = (bf16[3,256]{1,0:T(4,128)(2,1)}, bf16[3,256]{1,0:T(4,128)(2,1)}, u32[]{:S(2)}, u32[]{:S(2)}) collective-permute-start(bf16[3,256]{1,0:T(4,128)(2,1)} %slice.90), channel_id=1, source_target_pairs={{0,4},{4,8},{8,12},{12,16},{16,20},{20,24},{24,28},{1,5},{5,9},{9,... | collective-permute-start | bytes 4616 | tf_op jit(solution)/shard_map/ppermute | solution.py:16
  109.5 69.4 %all-gather.10.cloned.1.call-start = ((), (), s32[]{:S(2)}) async-start(), calls=%async_computation.5 | async-start | bytes 4718592 | tf_op jit(solution)/shard_map/all_gather | solution.py:21
  112.4 4.3 %collective-permute-start = (bf16[3,1024]{1,0:T(4,128)(2,1)S(1)}, bf16[3,1024]{1,0:T(4,128)(2,1)S(1)}, u32[]{:S(2)}, u32[]{:S(2)}) collective-permute-start(bf16[3,1024]{1,0:T(4,128)(2,1)S(1)} %slice.85), channel_id=1, source_target_pairs={{0,4},{4,8},{8,12},{12,16},{16,20},{20,24},{24,28},{1,5},{5,9},{9,... | collective-permute-start | bytes 18440 | tf_op jit(solution)/shard_map/ppermute | solution.py:16
  143.8 124.5 %reduce-scatter.2.cloned.1.call-start = ((), (), s32[]{:S(2)}) async-start(), calls=%async_computation.3 | async-start | bytes 2621440 | tf_op jit(solution)/shard_map/reduce_scatter | solution.py:141
  179.1 2.1 copy-start.1
  179.1 2.1 copy-start.6
  179.1 2.1 copy-start.14
  195.5 3.0 copy-start.3
  198.5 16.5 %copy-start.12 = (f32[1024]{0:T(1024)S(1)}, f32[1024]{0:T(1024)}, u32[]{:S(2)}) copy-start(f32[1024]{0:T(1024)} %param.29) | copy-start | bytes 12292
  219.8 79.5 %copy-start.5 = (bf16[512,1024]{1,0:T(8,128)(2,1)S(1)}, bf16[512,1024]{1,0:T(8,128)(2,1)}, u32[]{:S(2)}) copy-start(bf16[512,1024]{1,0:T(8,128)(2,1)} %param.17) | copy-start | bytes 3145732
  219.9 79.5 %all-gather.8.cloned.1.call-start = ((), (), s32[]{:S(2)}) async-start(), calls=%async_computation.4 | async-start | bytes 1310720 | tf_op jit(solution)/shard_map/all_gather | solution.py:144
Sparse Core Ops, SparseCore 0:
  11.3 88.9 all-reduce.1
  109.6 30.9 all-gather.5
  143.9 34.8 all-gather.9
  220.0 48.2 reduce-scatter.1
  270.2 29.1 all-gather.7
where the time goes:
time: 311 us; the launch traced here: 310 us
  waiting for transfers between devices  197 us (63%)
  matrix products  43.6 us (14%)
  blocking collectives  33.6 us (11%)
  between operations  13.4 us (4%)
  other arithmetic  9.56 us (3%)
  local copies, waits for them, and re-layouts  7.12 us (2%)
  starting transfers between devices  5.58 us (2%)
    psum x1, waiting for transfers between devices, on_device(): summed, total_squares = lax.psum((partial_value, local_squares), 'tp')  73.1 us
    reduce_scatter x1, waiting for transfers between devices, on_device(): lax.psum_scatter(contract_columns(out_down, normed), 'tp', scatter_dimens...  48.4 us
    all_gather x1, waiting for transfers between devices, on_device(): lax.all_gather(out_share, 'tp', axis=0, tiled=True)  29.3 us
    all_gather x1, waiting for transfers between devices, entering(): gathered = jax.tree.map(lambda a: lax.all_gather(a, axis), part)  24.7 us
    all_gather x1, waiting for transfers between devices, on_device(): state_all = lax.all_gather(state_act, 'tp', axis=1, tiled=True)  21 us
    dot_general x1, matrix products, on_device(): within = jnp.einsum('hts,shp->thp', mixing, values, precision=highest)  14.3 us
    psum x1, blocking collectives, on_device(): summed, total_squares = lax.psum((partial_value, local_squares), 'tp')  13.9 us
    psum x1, blocking collectives, on_device(): lax.psum(jnp.sum(gated * gated, axis=1)[:, None] * selector[None, :], 'tp')  11.8 us
  transfers between devices with their start and end apart: 7, of which 6 were waited for; matrix products, arithmetic and copies ran while one was open for 3% of the time, Pallas kernels for 0%

commit v1 on v0

--- a/solution.py
+++ b/solution.py
@@ -90,7 +90,10 @@
     rim_value, rim_state = shifted((value_pre[rim_start:], state_pre[rim_start:]), "seq", 1)
     value_act = depthwise(rim_value, value_pre, conv_value)
     state_act = depthwise(rim_state, state_pre, conv_state)
-    state_all = lax.all_gather(state_act, "tp", axis=1, tiled=True)
+    size = lax.axis_size("tp")
+    blocks = jnp.stack([state_act for _ in range(size)])
+    blocks = lax.all_to_all(blocks, "tp", split_axis=0, concat_axis=0)
+    state_all = jnp.concatenate(blocks, axis=1)
     heads_local = decay_log.shape[0]
     heads_total = heads_local * tp_count
     group_index = tp_index * heads_local // (heads_total // GROUPS)

time: 311 us -> 313 us (level)
  waiting for transfers between devices: 197 us -> 192 us
  starting transfers between devices: 5.58 us -> 9.78 us
  local copies, waits for them, and re-layouts: 7.12 us -> 10.6 us
    all_gather x1 -> x0, waiting for transfers between devices: 21 us -> none  [on_device(): state_all = lax.all_gather(state_act, 'tp', axis=1, tiled=True)]
    all_to_all x0 -> x1, waiting for transfers between devices: none -> 16.6 us  [on_device(): blocks = lax.all_to_all(blocks, 'tp', split_axis=0, concat_axis=0)]
    all_to_all x0 -> x1, starting transfers between devices: none -> 4.24 us  [on_device(): blocks = lax.all_to_all(blocks, 'tp', split_axis=0, concat_axis=0)]
where the time goes in v1:
time: 313 us; the launch traced here: 312 us
  waiting for transfers between devices  192 us (61%)
  matrix products  42.3 us (14%)
  blocking collectives  35.5 us (11%)
  between operations  13.4 us (4%)
  local copies, waits for them, and re-layouts  10.6 us (3%)
  starting transfers between devices  9.78 us (3%)
  other arithmetic  8.89 us (3%)
    psum x1, waiting for transfers between devices, on_device(): summed, total_squares = lax.psum((partial_value, local_squares), 'tp')  73.1 us
    reduce_scatter x1, waiting for transfers between devices, on_device(): lax.psum_scatter(contract_columns(out_down, normed), 'tp', scatter_dimens...  48.4 us
    all_gather x1, waiting for transfers between devices, on_device(): lax.all_gather(out_share, 'tp', axis=0, tiled=True)  29.3 us
    all_gather x1, waiting for transfers between devices, entering(): gathered = jax.tree.map(lambda a: lax.all_gather(a, axis), part)  23.7 us
    all_to_all x1, waiting for transfers between devices, on_device(): blocks = lax.all_to_all(blocks, 'tp', split_axis=0, concat_axis=0)  16.6 us
    dot_general x1, matrix products, on_device(): within = jnp.einsum('hts,shp->thp', mixing, values, precision=highest)  14.3 us
    psum x1, blocking collectives, on_device(): summed, total_squares = lax.psum((partial_value, local_squares), 'tp')  13.9 us
    psum x1, blocking collectives, on_device(): lax.psum(jnp.sum(gated * gated, axis=1)[:, None] * selector[None, :], 'tp')  11.8 us
  transfers between devices with their start and end apart: 7, of which 6 were waited for; matrix products, arithmetic and copies ran while one was open for 3% of the time, Pallas kernels for 0%

profile of v1, /device:TPU:0, one launch (start us, length us, event | category | flops | bytes accessed | tf_op | source)
XLA Modules:
  0.0 312.3 jit_solution(3207882419836768127)
XLA Ops:
  6.5 4.6 %fusion.29 = f32[512,1024]{1,0:T(8,128)} fusion(bf16[1024,1024]{1,0:T(8,128)(2,1)} %param.19, bf16[512,1024]{1,0:T(8,128)(2,1)} %param.17, f32[1024]{0:T(1024)} %param.18), kind=kOutput, calls=%fused_computation.51 | convolution fusion | flops 1075314688 | bytes 5246976 | tf_op jit(solution)/shard_map/dot_general | solution.py:78
  11.2 1.2 copy-done.6
  12.4 0.3 fusion.20
  12.7 13.9 %psum.22 = f32[512]{0:T(512)S(1)} all-reduce(f32[512]{0:T(512)S(1)} %fusion.20), channel_id=1, replica_groups=mesh['seq'=8,'tp'=4] {'tp'}, use_global_device_ids=true, to_apply=%region_2.0 | all-reduce | flops 512 | bytes 4096 | tf_op jit(solution)/shard_map/psum | solution.py:79
  26.6 0.6 fusion.57
  27.2 73.1 %all-reduce.2.cloned.1.call-done = f32[512,1024]{1,0:T(8,128)} async-done(((f32[512,1024]{1,0:T(8,128)}), f32[512,1024]{1,0:T(8,128)}) %all-reduce.2.cloned.1.call-update) | async-done | bytes 2097168 | tf_op jit(solution)/shard_map/psum | solution.py:79
  100.3 1.8 multiply_convert_fusion.2
  102.2 0.4 fusion.28
  102.6 0.1 compare_select_fusion.1
  102.7 0.4 convolution_convert_fusion.2
  103.1 0.6 slice.90
  103.7 2.0 collective-permute-start.1
  105.7 1.1 reduce-window.6
  106.8 0.2 slice_reduce_fusion
  107.0 0.7 maximum_convert_fusion.1
  107.8 1.0 multiply_convert_fusion.4
  108.8 1.1 stack.2
  109.9 4.2 %all-to-all-start = ((bf16[4,512,256]{2,1,0:T(8,128)(2,1)}), bf16[4,512,256]{2,1,0:T(8,128)(2,1)}, u32[]{:S(2)}, u32[]{:S(2)}) async-start(bf16[4,512,256]{2,1,0:T(8,128)(2,1)} %stack.2), calls=%async_computation | async-start | bytes 2097152 | tf_op jit(solution)/shard_map/all_to_all | solution.py:95
  114.2 2.8 convolution_convert_fusion.1
  117.0 3.4 %collective-permute-start = (bf16[3,1024]{1,0:T(4,128)(2,1)S(1)}, bf16[3,1024]{1,0:T(4,128)(2,1)S(1)}, u32[]{:S(2)}, u32[]{:S(2)}) collective-permute-start(bf16[3,1024]{1,0:T(4,128)(2,1)S(1)} %slice.85), channel_id=1, source_target_pairs={{0,4},{4,8},{8,12},{12,16},{16,20},{20,24},{24,28},{1,5},{5,9},{9,... | collective-permute-start | bytes 18440 | tf_op jit(solution)/shard_map/ppermute | solution.py:16
  120.5 0.1 copy_bitcast_fusion
  120.6 0.2 slice_reduce_fusion.1
  120.8 0.1 bitcast_exponential_fusion
  120.8 0.4 collective-permute-done
  121.3 0.3 maximum_convert_fusion
  121.6 1.3 multiply_convert_fusion.1
  122.9 1.3 copy.30
  124.2 16.6 %all-to-all-done = bf16[4,512,256]{2,1,0:T(8,128)(2,1)} async-done(((bf16[4,512,256]{2,1,0:T(8,128)(2,1)}), bf16[4,512,256]{2,1,0:T(8,128)(2,1)}, u32[]{:S(2)}, u32[]{:S(2)}) %all-to-all-start) | async-done | bytes 1048608 | tf_op jit(solution)/shard_map/all_to_all | solution.py:95
  140.8 1.4 copy.36
  142.1 1.0 copy-done.5
  143.1 2.0 fusion.13
  145.2 0.1 iota_compare_fusion
  145.3 9.9 %all-gather.1 = f32[8,1,16]{2,1,0:T(1,128)S(1)} all-gather(f32[1,1,16]{2,1,0:T(1,128)S(1)} %bitcast.106), channel_id=1, replica_groups=mesh['seq'=8,'tp'=4] {'seq'}, dimensions={0}, use_global_device_ids=true | all-gather | bytes 576 | tf_op jit(solution)/shard_map/all_gather | solution.py:21
  155.2 2.3 fusion.42
  157.4 23.7 %all-gather.7.cloned.1.call-done = f32[128,64,128]{2,1,0:T(8,128)} async-done(((f32[16,64,128]{2,1,0:T(8,128)}), f32[128,64,128]{2,1,0:T(8,128)}) %all-gather.7.cloned.1.call-update) | async-done | bytes 4194320 | tf_op jit(solution)/shard_map/all_gather | solution.py:21
  181.2 0.2 while.12
  181.4 2.0 fusion.39
  183.5 14.3 %fusion.14 = f32[512,16,64]{0,2,1:T(8,128)} fusion(bf16[512,16,64]{0,2,1:T(8,128)(2,1)S(1)} %bitcast.90, f32[512,16,64]{0,2,1:T(8,128)S(1)} %fusion.39, f32[16,512]{1,0:T(8,128)S(1)} %get-tuple-element.66, f32[16,512]{1,0:T(8,128)S(1)} %get-tuple-element.64, f32[512,512]{1,0:T(8,128)S(1)} %copy-done.8, pred[512,512]{1,0:T(8,128)(4,1)S(1)} %iota_compare_fusion, ...), kind=kOutput, calls=%fused_computation.23 | convolution fusion | flops 3244818432 | bytes 6651968 | tf_op jit(solution)/shard_map/hts,shp->thp/dot_general | solution.py:115
  197.8 3.0 copy.34
  200.8 4.5 %multiply_reduce_fusion = (f32[512]{0:T(512)S(1)}, f32[512,1024]{1,0:T(8,128)}) fusion(f32[512,1024]{1,0:T(8,128)} %copy.34, bf16[512,1024]{1,0:T(8,128)(2,1)S(1)} %copy-done.4, bf16[1024,1024]{1,0:T(8,128)(2,1)S(1)} %copy-done), kind=kOutput, calls=%fused_computation.40 | convolution fusion | flops 1078459904 | bytes 7342080 | tf_op jit(solution)/shard_map/dot_general | solution.py:83
  205.3 0.1 broadcast_multiply_fusion
  205.4 11.8 %psum.23 = f32[512,4]{0,1:T(4,128)S(1)} all-reduce(f32[512,4]{0,1:T(4,128)S(1)} %broadcast_multiply_fusion), channel_id=1, replica_groups=mesh['seq'=8,'tp'=4] {'tp'}, use_global_device_ids=true, to_apply=%region_8.9 | all-reduce | flops 2048 | bytes 16384 | tf_op jit(solution)/shard_map/psum | solution.py:139
  217.2 0.1 multiply_reduce_fusion.1
  217.3 4.8 %convolution_bitcast_fusion = f32[1024,512]{0,1:T(8,128)} fusion(bf16[1024,1024]{1,0:T(8,128)(2,1)} %param.30, f32[512,1024]{1,0:T(8,128)} %get-tuple-element.77, f32[1024]{0:T(1024)S(1)} %copy-done.14, f32[512]{0:T(512)S(1)} %add_rsqrt_fusion), kind=kOutput, calls=%fused_computation.43 | convolution fusion | flops 1075314688 | bytes 6297600 | tf_op jit(solution)/shard_map/dot_general | solution.py:39
  222.2 48.4 %reduce-scatter.2.cloned.1.call-done = f32[256,512]{0,1:T(8,128)} async-done(((f32[1024,512]{0,1:T(8,128)}), f32[256,512]{0,1:T(8,128)}) %reduce-scatter.2.cloned.1.call-update) | async-done | bytes 524304 | tf_op jit(solution)/shard_map/reduce_scatter | solution.py:144
  270.6 1.8 convert_element_type.79
  272.4 29.3 %all-gather.5.cloned.1.call-done = bf16[1024,512]{0,1:T(8,128)(2,1)} async-done(((bf16[256,512]{0,1:T(8,128)(2,1)}), bf16[1024,512]{0,1:T(8,128)(2,1)}) %all-gather.5.cloned.1.call-update) | async-done | bytes 1048592 | tf_op jit(solution)/shard_map/all_gather | solution.py:147
  301.7 4.1 %fusion.21 = bf16[512,1024]{1,0:T(8,128)(2,1)} fusion(bf16[512,1024]{1,0:T(8,128)(2,1)S(1)} %copy-done.7, bf16[1024,512]{0,1:T(8,128)(2,1)} %all-gather.5.cloned.1.call-done, bf16[1024,1024]{1,0:T(8,128)(2,1)} %param.31), kind=kOutput, calls=%fused_computation.30 | convolution fusion | flops 1075314688 | bytes 5242880 | tf_op jit(solution)/shard_map/dot_general | solution.py:33
  (51 shorter events, 0.4 us)
Async XLA Ops:
  6.5 194.3 %copy-start = (bf16[1024,1024]{1,0:T(8,128)(2,1)S(1)}, bf16[1024,1024]{1,0:T(8,128)(2,1)}, u32[]{:S(2)}) copy-start(bf16[1024,1024]{1,0:T(8,128)(2,1)} %param.20) | copy-start | bytes 6291460
  6.5 93.8 %all-reduce.2.cloned.1.call-start = ((), (), s32[]{:S(2)}) async-start(), calls=%async_computation.2 | async-start | bytes 4194304 | tf_op jit(solution)/shard_map/psum | solution.py:79
  11.2 1.2 copy-start.6
  11.2 15.4 %copy-start.15 = (f32[16]{0:T(128)S(1)}, f32[16]{0:T(128)}, u32[]{:S(2)}) copy-start(f32[16]{0:T(128)} %param.27) | copy-start | bytes 196
  11.2 15.4 %copy-start.11 = (f32[4,256]{1,0:T(4,128)S(1)}, f32[4,256]{1,0:T(4,128)}, u32[]{:S(2)}) copy-start(f32[4,256]{1,0:T(4,128)} %param.25) | copy-start | bytes 12292
  11.2 16.0 %copy-start.10 = (f32[4,1024]{1,0:T(4,128)S(1)}, f32[4,1024]{1,0:T(4,128)}, u32[]{:S(2)}) copy-start(f32[4,1024]{1,0:T(4,128)} %param.24) | copy-start | bytes 49156
  12.4 89.8 %copy-start.9 = (bf16[1024,16]{0,1:T(8,128)(2,1)S(1)}, bf16[1024,16]{0,1:T(8,128)(2,1)}, u32[]{:S(2)}) copy-start(bf16[1024,16]{0,1:T(8,128)(2,1)} %param.23) | copy-start | bytes 98308
  12.4 89.8 %copy-start.12 = (f32[16]{0:T(128)S(1)}, f32[16]{0:T(128)}, u32[]{:S(2)}) copy-start(f32[16]{0:T(128)} %param.26) | copy-start | bytes 196
  100.3 2.3 copy-start.13
  102.2 12.0 %copy-start.3 = (bf16[512,1024]{1,0:T(8,128)(2,1)}, bf16[512,1024]{1,0:T(8,128)(2,1)S(1)}, u32[]{:S(2)}) copy-start(bf16[512,1024]{1,0:T(8,128)(2,1)S(1)} %multiply_convert_fusion.2) | copy-start | bytes 3145732
  103.7 3.3 %collective-permute-start.1 = (bf16[3,256]{1,0:T(4,128)(2,1)}, bf16[3,256]{1,0:T(4,128)(2,1)}, u32[]{:S(2)}, u32[]{:S(2)}) collective-permute-start(bf16[3,256]{1,0:T(4,128)(2,1)} %slice.90), channel_id=1, source_target_pairs={{0,4},{4,8},{8,12},{12,16},{16,20},{20,24},{24,28},{1,5},{5,9},{9,... | collective-permute-start | bytes 4616 | tf_op jit(solution)/shard_map/ppermute | solution.py:16
  109.9 30.9 %all-to-all-start = ((bf16[4,512,256]{2,1,0:T(8,128)(2,1)}), bf16[4,512,256]{2,1,0:T(8,128)(2,1)}, u32[]{:S(2)}, u32[]{:S(2)}) async-start(bf16[4,512,256]{2,1,0:T(8,128)(2,1)} %stack.2), calls=%async_computation | async-start | bytes 2097152 | tf_op jit(solution)/shard_map/all_to_all | solution.py:95
  114.1 67.0 %all-gather.7.cloned.1.call-start = ((), (), s32[]{:S(2)}) async-start(), calls=%async_computation.5 | async-start | bytes 4718592 | tf_op jit(solution)/shard_map/all_gather | solution.py:21
  117.0 4.2 %collective-permute-start = (bf16[3,1024]{1,0:T(4,128)(2,1)S(1)}, bf16[3,1024]{1,0:T(4,128)(2,1)S(1)}, u32[]{:S(2)}, u32[]{:S(2)}) collective-permute-start(bf16[3,1024]{1,0:T(4,128)(2,1)S(1)} %slice.85), channel_id=1, source_target_pairs={{0,4},{4,8},{8,12},{12,16},{16,20},{20,24},{24,28},{1,5},{5,9},{9,... | collective-permute-start | bytes 18440 | tf_op jit(solution)/shard_map/ppermute | solution.py:16
  124.2 18.9 %copy-start.1 = (bf16[512,1024]{0,1:T(8,128)(2,1)S(1)}, bf16[512,1024]{0,1:T(8,128)(2,1)}, u32[]{:S(2)}) copy-start(bf16[512,1024]{0,1:T(8,128)(2,1)} %copy.30) | copy-start | bytes 3145732
  142.1 1.0 copy-start.5
  145.1 125.5 %reduce-scatter.2.cloned.1.call-start = ((), (), s32[]{:S(2)}) async-start(), calls=%async_computation.3 | async-start | bytes 2621440 | tf_op jit(solution)/shard_map/reduce_scatter | solution.py:144
  181.4 2.1 copy-start.2
  181.4 2.1 copy-start.8
  181.4 2.1 copy-start.16
  197.8 3.0 copy-start.4
  200.8 16.5 %copy-start.14 = (f32[1024]{0:T(1024)S(1)}, f32[1024]{0:T(1024)}, u32[]{:S(2)}) copy-start(f32[1024]{0:T(1024)} %param.29) | copy-start | bytes 12292
  222.2 79.5 %copy-start.7 = (bf16[512,1024]{1,0:T(8,128)(2,1)S(1)}, bf16[512,1024]{1,0:T(8,128)(2,1)}, u32[]{:S(2)}) copy-start(bf16[512,1024]{1,0:T(8,128)(2,1)} %param.17) | copy-start | bytes 3145732
  222.2 79.5 %all-gather.5.cloned.1.call-start = ((), (), s32[]{:S(2)}) async-start(), calls=%async_computation.4 | async-start | bytes 1310720 | tf_op jit(solution)/shard_map/all_gather | solution.py:147
Sparse Core Ops, SparseCore 0:
  11.3 88.9 all-reduce.1
  145.2 35.8 all-gather.6
  222.3 48.2 reduce-scatter.1
  272.5 29.1 all-gather.4
